TPU v7x, 32 devices: a whole 2x2x4 slice. The times are simulated.
32 devices in a mesh: owner: 4 (over y, core), rows: 8 (over z, x).
Axes of the slice: x: 2, y: 2, z: 4, core: 2. Of those that a mesh axis runs over, the one named last changes fastest.
Arguments:
- train_gate: float32 [128, 2048, 768], P('owner', 'rows'), may hold values from -0.125 to 0.125
- train_up: float32 [128, 2048, 768], P('owner', 'rows'), may hold values from -0.125 to 0.125
- router_weight: float32 [2048, 128], P('rows', 'owner'), may hold values from -0.125 to 0.125
- router_gain: float32 [2048], P('rows'), may hold values from 0.25 to 1.75
Outputs:
- ready_gate: bfloat16 [128, 768, 2048], P(('owner', 'rows'))
- ready_up: bfloat16 [128, 768, 2048], P(('owner', 'rows'))
- serve_router: bfloat16 [2048, 128], replicated
All inputs are finite; a program needn't handle non-finite values.
Results may differ from a plain program's by a relative error of at most 0.001.
Values may be sent and summed in bfloat16 or wider, within the bound.
A program may use at most 192 MiB of HBM per device.

v0:
```python
import jax
import jax.numpy as jnp
from jax import lax
from jax.sharding import PartitionSpec as P


def on_device(train_gate, train_up, router_weight, router_gain):
    narrow_gate, narrow_up = (train_gate.astype(jnp.bfloat16), train_up.astype(jnp.bfloat16))
    ready_gate, ready_up = (
        lax.all_to_all(narrow_gate, "rows", split_axis=0, concat_axis=1, tiled=True),
        lax.all_to_all(narrow_up, "rows", split_axis=0, concat_axis=1, tiled=True),
    )
    ready_gate = jnp.transpose(ready_gate, (0, 2, 1))
    ready_up = jnp.transpose(ready_up, (0, 2, 1))
    part_router = (router_weight * router_gain[:, None]).astype(jnp.bfloat16)
    row_router = lax.all_gather(part_router, "rows", axis=0, tiled=True)
    serve_router = lax.all_gather(row_router, "owner", axis=1, tiled=True)
    return (ready_gate, ready_up, serve_router)


def solution(mesh):
    placed = (P("owner", "rows", None), P("owner", "rows", None), P("rows", "owner"), P("rows"))
    return jax.shard_map(
        on_device,
        mesh=mesh,
        in_specs=placed,
        out_specs=(P(("owner", "rows"), None, None), P(("owner", "rows"), None, None), P()),
        check_vma=False,
    )
```

profile of v0, /device:TPU:10, one launch (start us, length us, event | category | flops | bytes accessed | tf_op | source)
XLA Modules:
  0.0 668.3 jit_solution(13268045616997217038)
XLA Ops:
  0.6 13.2 %convert_element_type.9 = bf16[32,256,768]{2,1,0:T(8,128)(2,1)} convert(f32[32,256,768]{2,1,0:T(8,128)} %param.4) | non-fusion elementwise | flops 6291456 | bytes 37748736 | tf_op jit(solution)/shard_map/convert_element_type | solution.py:8
  13.8 6.2 all-to-all-start
  20.0 13.4 %convert_element_type.10 = bf16[32,256,768]{2,1,0:T(8,128)(2,1)} convert(f32[32,256,768]{2,1,0:T(8,128)} %param.5) | non-fusion elementwise | flops 6291456 | bytes 37748736 | tf_op jit(solution)/shard_map/convert_element_type | solution.py:8
  33.4 0.0 copy-start
  33.4 0.0 copy-start.1
  33.4 256.3 %all-to-all-done = bf16[32,256,768]{2,1,0:T(8,128)(2,1)} async-done(((bf16[32,256,768]{2,1,0:T(8,128)(2,1)}), bf16[32,256,768]{2,1,0:T(8,128)(2,1)}, u32[]{:S(2)}, u32[]{:S(2)}) %all-to-all-start) | async-done | bytes 12582944 | tf_op jit(solution)/shard_map/all_to_all | solution.py:10
  289.7 8.6 %all-to-all-start.1 = ((bf16[32,256,768]{2,1,0:T(8,128)(2,1)}), bf16[32,256,768]{2,1,0:T(8,128)(2,1)}, u32[]{:S(2)}, u32[]{:S(2)}) async-start(bf16[32,256,768]{2,1,0:T(8,128)(2,1)} %convert_element_type.10), calls=%async_computation.1 | async-start | bytes 25165824 | tf_op jit(solution)/shard_map/all_to_all | solution.py:11
  298.3 0.0 copy-done
  298.3 0.0 copy-done.1
  298.4 289.0 %all_gather.6 = bf16[2048,32]{0,1:T(8,128)(2,1)S(1)} all-gather(bf16[256,32]{0,1:T(8,128)(2,1)S(1)} %multiply_convert_fusion), channel_id=1, replica_groups=mesh['owner'=4,'rows'=8] {'rows'}, dimensions={0}, use_global_device_ids=true | all-gather | bytes 147456 | tf_op jit(solution)/shard_map/all_gather | solution.py:16
  587.4 7.2 %all_gather.7 = bf16[2048,128]{0,1:T(8,128)(2,1)S(1)} all-gather(bf16[2048,32]{0,1:T(8,128)(2,1)S(1)} %all_gather.6), channel_id=1, replica_groups=mesh['owner'=4,'rows'=8] {'owner'}, dimensions={1}, use_global_device_ids=true | all-gather | bytes 655360 | tf_op jit(solution)/shard_map/all_gather | solution.py:17
  594.6 1.0 copy.12
  595.6 16.9 %copy.10 = bf16[8,4,256,768]{2,0,3,1:T(8,128)(2,1)} copy(bf16[8,4,256,768]{3,2,1,0:T(8,128)(2,1)} %bitcast) | data formatting | bytes 25165824 | tf_op jit(solution)/shard_map/all_to_all | solution.py:10
  612.5 19.5 %all_to_all.29 = bf16[4,2048,768]{1,2,0:T(8,128)(2,1)} reshape(bf16[4,8,256,768]{2,1,3,0:T(8,128)(2,1)} %bitcast.14) | data formatting | bytes 25165824 | tf_op jit(solution)/shard_map/all_to_all | solution.py:10
  631.9 0.0 all-to-all-done.1
  631.9 16.9 %copy.11 = bf16[8,4,256,768]{2,0,3,1:T(8,128)(2,1)} copy(bf16[8,4,256,768]{3,2,1,0:T(8,128)(2,1)} %bitcast.3) | data formatting | bytes 25165824 | tf_op jit(solution)/shard_map/all_to_all | solution.py:11
  648.8 19.5 %all_to_all.33 = bf16[4,2048,768]{1,2,0:T(8,128)(2,1)} reshape(bf16[4,8,256,768]{2,1,3,0:T(8,128)(2,1)} %bitcast.15) | data formatting | bytes 25165824 | tf_op jit(solution)/shard_map/all_to_all | solution.py:11
  (1 shorter events, 0.0 us)
Async XLA Ops:
  13.8 275.9 %all-to-all-start = ((bf16[32,256,768]{2,1,0:T(8,128)(2,1)}), bf16[32,256,768]{2,1,0:T(8,128)(2,1)}, u32[]{:S(2)}, u32[]{:S(2)}) async-start(bf16[32,256,768]{2,1,0:T(8,128)(2,1)} %convert_element_type.9), calls=%async_computation | async-start | bytes 25165824 | tf_op jit(solution)/shard_map/all_to_all | solution.py:10
  33.4 264.9 %copy-start = (f32[256,32]{0,1:T(8,128)S(1)}, f32[256,32]{0,1:T(8,128)}, u32[]{:S(2)}) copy-start(f32[256,32]{0,1:T(8,128)} %param.6) | copy-start | bytes 98308
  33.4 264.9 %copy-start.1 = (f32[256]{0:T(256)S(1)}, f32[256]{0:T(256)}, u32[]{:S(2)}) copy-start(f32[256]{0:T(256)} %param.7) | copy-start | bytes 3076
  289.7 342.2 %all-to-all-start.1 = ((bf16[32,256,768]{2,1,0:T(8,128)(2,1)}), bf16[32,256,768]{2,1,0:T(8,128)(2,1)}, u32[]{:S(2)}, u32[]{:S(2)}) async-start(bf16[32,256,768]{2,1,0:T(8,128)(2,1)} %convert_element_type.10), calls=%async_computation.1 | async-start | bytes 25165824 | tf_op jit(solution)/shard_map/all_to_all | solution.py:11
where the time goes:
time: 675 us; the launch traced here: 668 us
  blocking collectives  296 us (44%)
  waiting for transfers between devices  256 us (38%)
  local copies, waits for them, and re-layouts  73.7 us (11%)
  other arithmetic  26.6 us (4%)
  starting transfers between devices  14.8 us (2%)
    all_gather x1, blocking collectives, on_device(): row_router = lax.all_gather(part_router, 'rows', axis=0, tiled=True)  289 us
    all_to_all x1, waiting for transfers between devices, on_device(): lax.all_to_all(narrow_gate, 'rows', split_axis=0, concat_axis=1, tiled=True)  256 us
    all_to_all x2, local copies, waits for them, and re-layouts, on_device(): lax.all_to_all(narrow_up, 'rows', split_axis=0, concat_axis=1, tiled=True)  36.4 us
    all_to_all x2, local copies, waits for them, and re-layouts, on_device(): lax.all_to_all(narrow_gate, 'rows', split_axis=0, concat_axis=1, tiled=True)  36.3 us
  transfers between devices with their start and end apart: 2, of which 1 were waited for; matrix products, arithmetic and copies ran while one was open for 5% of the time, Pallas kernels for 0%

commit v1 on v0

v1 whole, which is shorter than its diff:
```python
import functools

import jax
import jax.numpy as jnp
from jax import lax
from jax.experimental import pallas as pl
from jax.experimental.pallas import tpu as pltpu
from jax.sharding import PartitionSpec as P

STAGES = 4
LANES = 128


def targets_of(n):
    half, quarter = n // 2, max(n // 4, 1)
    table = []
    for r in range(n):
        others = [t for t in range(n) if t != r]
        near = [t for t in others if (t < half) == (r < half)]
        far = [t for t in others if t not in near]
        outer = r // quarter in (0, (n - 1) // quarter)
        if outer:
            order = near + far
        else:
            order = []
            near, far = list(near), list(far)
            while near or far:
                order += far[:1] + near[:1]
                near, far = near[1:], far[1:]
        table.append((order, outer))
    return table


def pick(values, index):
    result = jnp.int32(values[0])
    for place, value in enumerate(values[1:], 1):
        result = jnp.where(index == place, jnp.int32(value), result)
    return result


def kernel(
    n, owners, gate, up, router, gain, out_gate, out_up, out_router,
    stage, sent, row_router, stage_sem, send_sem, recv_sem,
    row_send, row_recv, owner_send, owner_recv,
):
    me = lax.axis_index("rows")
    my_owner = lax.axis_index("owner")
    width, each = gate.shape[1], gate.shape[0] // n
    wide = router.shape[0]
    chunks = 2 * each
    remote = (n - 1) * chunks
    total = n * chunks
    table = targets_of(n)
    outer = pick([int(o) for _, o in table], me) == 1

    def place(step):
        by_target = step // chunks
        order = jnp.where(outer, by_target, step % (n - 1))
        chunk = jnp.where(outer, step % chunks, step // (n - 1))
        target = jnp.int32(0)
        for s in range(n - 1):
            target = jnp.where(order == s, pick([o[s] for o, _ in table], me), target)
        own = step >= remote
        target = jnp.where(own, me, target)
        chunk = jnp.where(own, step - remote, chunk)
        return target, chunk

    def load(step):
        target, chunk = place(step)
        slot = step % STAGES
        for index, source in enumerate((gate, up)):

            @pl.when(chunk // each == index)
            def _():
                pltpu.make_async_copy(
                    source.at[target * each + chunk % each], stage.at[slot], stage_sem.at[slot]
                ).start()

    def narrow(slot):
        pltpu.make_async_copy(gate.at[0], stage.at[slot], stage_sem.at[slot]).wait()
        return stage[slot].astype(jnp.bfloat16).T

    for step in range(STAGES):
        load(jnp.int32(step))

    barrier = pltpu.get_barrier_semaphore()
    for d in range(1, n):
        pl.semaphore_signal(barrier, inc=1, device_id={"rows": lax.rem(me + d, n)})
    for d in range(1, owners):
        pl.semaphore_signal(barrier, inc=1, device_id={"owner": lax.rem(my_owner + d, owners)})
    pl.semaphore_wait(barrier, n - 1 + owners - 1)

    columns = pl.ds(pl.multiple_of(me * width, width), width)

    def remote_step(step, carry):
        target, chunk = place(step)
        slot = step % STAGES
        sent[step] = narrow(slot)
        load(step + STAGES)
        for index, out in enumerate((out_gate, out_up)):

            @pl.when(chunk // each == index)
            def _():
                pltpu.make_async_remote_copy(
                    src_ref=sent.at[step],
                    dst_ref=out.at[chunk % each, :, columns],
                    send_sem=send_sem.at[step],
                    recv_sem=recv_sem.at[me * chunks + chunk],
                    device_id={"rows": target},
                ).start()

        return carry

    lax.fori_loop(0, 1, remote_step, 0)

    row_router[:, columns] = (router[...] * gain[...]).astype(jnp.bfloat16)

    def row_copy(d, source):
        span = pl.ds(pl.multiple_of(source * width, width), width)
        return pltpu.make_async_remote_copy(
            src_ref=row_router.at[:, span],
            dst_ref=row_router.at[:, span],
            send_sem=row_send.at[d],
            recv_sem=row_recv.at[d],
            device_id={"rows": lax.rem(me + d, n)},
        )

    for d in range(1, n):
        row_copy(d, me).start()

    lax.fori_loop(1, remote, remote_step, 0)

    def own_step(step, carry):
        chunk = step - remote
        mine = narrow(step % STAGES)

        @pl.when(step + STAGES < total)
        def _():
            load(step + STAGES)

        for index, out in enumerate((out_gate, out_up)):

            @pl.when(chunk // each == index)
            def _():
                out[chunk % each, :, columns] = mine

        return carry

    lax.fori_loop(remote, total, own_step, 0)

    for d in range(1, n):
        row_copy(d, lax.rem(me + n - d, n)).wait_recv()
        row_copy(d, me).wait_send()
    owned = pl.ds(pl.multiple_of(my_owner * wide, wide), wide)
    out_router[owned, :] = row_router[...]
    owner_copies = [
        pltpu.make_async_remote_copy(
            src_ref=row_router,
            dst_ref=out_router.at[owned, :],
            send_sem=owner_send.at[d],
            recv_sem=owner_recv.at[d],
            device_id={"owner": lax.rem(my_owner + d, owners)},
        )
        for d in range(1, owners)
    ]
    for copy in owner_copies:
        copy.start()
    for copy in owner_copies:
        copy.wait()

    def chunk_copy(send, recv):
        return pltpu.make_async_remote_copy(
            src_ref=sent.at[0],
            dst_ref=out_gate.at[0, :, columns],
            send_sem=send_sem.at[send],
            recv_sem=recv_sem.at[recv],
            device_id={"rows": lax.rem(me + 1, n)},
        )

    def drain(step, carry):
        source = lax.rem(me + 1 + step // chunks, n)
        chunk_copy(step, source * chunks + step % chunks).wait_recv()
        chunk_copy(step, 0).wait_send()
        return carry

    lax.fori_loop(0, remote, drain, 0)


def exchange(n, owners, train_gate, train_up, router_weight, router_gain):
    experts, width, inner = train_gate.shape
    each, wide = experts // n, router_weight.shape[1]
    chunks = 2 * each
    ready = pltpu.VMEM((each, inner, n * width), jnp.bfloat16)
    dma = pltpu.SemaphoreType.DMA
    vmem = pl.BlockSpec(memory_space=pltpu.VMEM)
    hbm = pl.BlockSpec(memory_space=pl.ANY)
    ready_gate, ready_up, router = pl.pallas_call(
        functools.partial(kernel, n, owners),
        out_shape=(ready, ready, pltpu.VMEM((owners * wide, n * width), jnp.bfloat16)),
        in_specs=[hbm, hbm, vmem, vmem],
        out_specs=(vmem, vmem, vmem),
        scratch_shapes=[
            pltpu.VMEM((STAGES, width, inner), jnp.float32),
            pltpu.VMEM(((n - 1) * chunks, inner, width), jnp.bfloat16),
            pltpu.VMEM((wide, n * width), jnp.bfloat16),
            dma((STAGES,)),
            dma(((n - 1) * chunks,)),
            dma((n * chunks,)),
            dma((n,)),
            dma((n,)),
            dma((owners,)),
            dma((owners,)),
        ],
        compiler_params=pltpu.CompilerParams(
            collective_id=0, has_side_effects=True, vmem_limit_bytes=KERNEL_VMEM
        ),
    )(train_gate, train_up, router_weight.T, router_gain[None, :])
    ready_gate, ready_up = put_out(ready_gate, ready_up)
    return ready_gate, ready_up, router.T


def put_out(*arrays):
    def body(*refs):
        sources, outs, sem = refs[: len(arrays)], refs[len(arrays) : -1], refs[-1]
        copies = [
            pltpu.make_async_copy(source.at[part], out.at[part], sem.at[index, part])
            for index, (source, out) in enumerate(zip(sources, outs))
            for part in range(source.shape[0])
        ]
        for copy in copies:
            copy.start()
        for copy in copies:
            copy.wait()

    return pl.pallas_call(
        body,
        out_shape=[jax.ShapeDtypeStruct(a.shape, a.dtype) for a in arrays],
        in_specs=[pl.BlockSpec(memory_space=pltpu.VMEM)] * len(arrays),
        out_specs=[pl.BlockSpec(memory_space=pl.ANY)] * len(arrays),
        scratch_shapes=[pltpu.SemaphoreType.DMA((len(arrays), arrays[0].shape[0]))],
        compiler_params=pltpu.CompilerParams(vmem_limit_bytes=1024 * 1024),
    )(*[pltpu.with_memory_space_constraint(a, pltpu.VMEM) for a in arrays])


KERNEL_VMEM = 32 * 1024 * 1024


def plain(train_gate, train_up, router_weight, router_gain):
    narrow_gate, narrow_up = (train_gate.astype(jnp.bfloat16), train_up.astype(jnp.bfloat16))
    ready_gate, ready_up = (
        lax.all_to_all(narrow_gate, "rows", split_axis=0, concat_axis=1, tiled=True),
        lax.all_to_all(narrow_up, "rows", split_axis=0, concat_axis=1, tiled=True),
    )
    ready_gate = jnp.transpose(ready_gate, (0, 2, 1))
    ready_up = jnp.transpose(ready_up, (0, 2, 1))
    part_router = (router_weight * router_gain[:, None]).astype(jnp.bfloat16)
    row_router = lax.all_gather(part_router, "rows", axis=0, tiled=True)
    serve_router = lax.all_gather(row_router, "owner", axis=1, tiled=True)
    return ready_gate, ready_up, serve_router


def solution(mesh):
    n, owners = mesh.shape["rows"], mesh.shape["owner"]

    def on_device(train_gate, train_up, router_weight, router_gain):
        if n > 1 and owners > 1 and train_gate.shape[1] % LANES == 0 and router_weight.shape[1] % 16 == 0:
            return exchange(n, owners, train_gate, train_up, router_weight, router_gain)
        return plain(train_gate, train_up, router_weight, router_gain)

    placed = (P("owner", "rows", None), P("owner", "rows", None), P("rows", "owner"), P("rows"))
    return jax.shard_map(
        on_device,
        mesh=mesh,
        in_specs=placed,
        out_specs=(P(("owner", "rows"), None, None), P(("owner", "rows"), None, None), P()),
        check_vma=False,
    )
```

time: 675 us -> 574 us (0.85)
  Pallas kernels: 0 us -> 571 us
  blocking collectives: 296 us -> 0 us
  waiting for transfers between devices: 256 us -> 0 us
  local copies, waits for them, and re-layouts: 73.7 us -> 1 us
  other arithmetic: 26.6 us -> 0 us
  starting transfers between devices: 14.8 us -> 0 us
    pallas_call x0 -> x2, Pallas kernels: none -> 571 us  [the longest x1 563 us: exchange(): pl.pallas_call(functools.partial(kernel, n, owners), out_shape=(ready, re...]
    all_gather x2 -> x0, blocking collectives: 296 us -> none  [the longest x1 289 us: on_device(): row_router = lax.all_gather(part_router, 'rows', axis=0, tiled=True)]
    all_to_all x2 -> x0, waiting for transfers between devices: 256 us -> none  [the longest x1 256 us: on_device(): lax.all_to_all(narrow_gate, 'rows', split_axis=0, concat_axis=1, tiled=True)]
    all_to_all x4 -> x0, local copies, waits for them, and re-layouts: 72.7 us -> none  [the longest x2 36.4 us: on_device(): lax.all_to_all(narrow_up, 'rows', split_axis=0, concat_axis=1, tiled=True)]
    convert_element_type x3 -> x0, other arithmetic: 26.6 us -> none  [the longest x1 13.4 us: on_device(): train_up.astype(jnp.bfloat16)]
    all_to_all x2 -> x0, starting transfers between devices: 14.8 us -> none  [the longest x1 8.61 us: on_device(): lax.all_to_all(narrow_up, 'rows', split_axis=0, concat_axis=1, tiled=True)]
  transfers between devices with their start and end apart: 2 -> 0, of which waited for: 1 -> 0; matrix products, arithmetic and copies ran while one was open for 5% -> 0% of each run, Pallas kernels for 0% -> 0%
where the time goes in v1:
time: 574 us; the launch traced here: 573 us
  Pallas kernels  571 us (99%)
    pallas_call x1, Pallas kernels, exchange(): pl.pallas_call(functools.partial(kernel, n, owners), out_shape=(ready, re...  563 us

profile of v1, /device:TPU:10, one launch (start us, length us, event | category | flops | bytes accessed | tf_op | source)
XLA Modules:
  0.0 573.1 jit_solution(11655171124449690397)
XLA Ops:
  0.6 562.9 %shard_map.67 = (bf16[4,768,2048]{2,1,0:T(8,128)(2,1)S(1)}, bf16[4,768,2048]{2,1,0:T(8,128)(2,1)S(1)}, bf16[128,2048]{1,0:T(8,128)(2,1)S(1)}) custom-call(f32[32,256,768]{2,1,0:T(8,128)} %gate.1, f32[32,256,768]{2,1,0:T(8,128)} %up.1, f32[32,256]{1,0:T(8,128)} %bitcast.4, f32[1,256]{1,0:T(1,128)} %bitcast.5), custom_call_target="tpu_custom_call" | custom-call | tf_op jit(solution)/shard_map/pallas_call | solution.py:197
  563.5 8.5 %shard_map.68 = (bf16[4,768,2048]{2,1,0:T(8,128)(2,1)}, bf16[4,768,2048]{2,1,0:T(8,128)(2,1)}) custom-call(bf16[4,768,2048]{2,1,0:T(8,128)(2,1)S(1)} %get-tuple-element.8.refs_0_, bf16[4,768,2048]{2,1,0:T(8,128)(2,1)S(1)} %get-tuple-element.9.refs_1_), custom_call_target="tpu_custom_call" | custom-call | tf_op jit(solution)/shard_map/pallas_call | solution.py:235
  572.1 1.0 copy.7

commit v2 on v1

--- a/solution.py
+++ b/solution.py
@@ -15,7 +15,10 @@
     half, quarter = n // 2, max(n // 4, 1)
     table = []
     for r in range(n):
-        others = [t for t in range(n) if t != r]
+        others = sorted(
+            (t for t in range(n) if t != r),
+            key=lambda t: (-abs(t // quarter - r // quarter), -((t - r) % quarter)),
+        )
         near = [t for t in others if (t < half) == (r < half)]
         far = [t for t in others if t not in near]
         outer = r // quarter in (0, (n - 1) // quarter)

time: 574 us -> 573 us (level)
  no operation moved by 1% of the time
where the time goes in v2:
time: 573 us
  Pallas kernels  571 us (100%)
    pallas_call x1, Pallas kernels, exchange(): pl.pallas_call(functools.partial(kernel, n, owners), out_shape=(ready, re...  563 us

profile of v2, /device:TPU:10, one launch (start us, length us, event | category | flops | bytes accessed | tf_op | source)
XLA Modules:
  0.0 573.1 jit_solution(13786581018159826874)
XLA Ops:
  0.6 562.9 %shard_map.67 = (bf16[4,768,2048]{2,1,0:T(8,128)(2,1)S(1)}, bf16[4,768,2048]{2,1,0:T(8,128)(2,1)S(1)}, bf16[128,2048]{1,0:T(8,128)(2,1)S(1)}) custom-call(f32[32,256,768]{2,1,0:T(8,128)} %gate.1, f32[32,256,768]{2,1,0:T(8,128)} %up.1, f32[32,256]{1,0:T(8,128)} %bitcast.4, f32[1,256]{1,0:T(1,128)} %bitcast.5), custom_call_target="tpu_custom_call" | custom-call | tf_op jit(solution)/shard_map/pallas_call | solution.py:200
  563.5 8.5 %shard_map.68 = (bf16[4,768,2048]{2,1,0:T(8,128)(2,1)}, bf16[4,768,2048]{2,1,0:T(8,128)(2,1)}) custom-call(bf16[4,768,2048]{2,1,0:T(8,128)(2,1)S(1)} %get-tuple-element.8.refs_0_, bf16[4,768,2048]{2,1,0:T(8,128)(2,1)S(1)} %get-tuple-element.9.refs_1_), custom_call_target="tpu_custom_call" | custom-call | tf_op jit(solution)/shard_map/pallas_call | solution.py:238
  572.1 1.0 copy.7
